TPU v7x, 32 devices: a whole 2x2x4 slice. The times are simulated.
32 devices in a mesh: dom: 16 (over z, y, x), field: 2 (over core).
Axes of the slice: x: 2, y: 2, z: 4, core: 2. Of those that a mesh axis runs over, the one named last changes fastest.
Arguments:
- ocean: bfloat16 [30, 32768], P('field', 'dom'), may hold values from -6 to 6
- grad_weight: bfloat16 [256, 4, 128, 256], P('dom'), may hold values from -0.25 to 0.25
- neighbours: int32 [256, 4], P('dom'), may hold values from 0 to 255, as said below
- remap_weight: bfloat16 [2048, 384, 128], P(('dom', 'field')), may hold values from -0.109375 to 0.109375
- tile_src: int32 [2048], P(('dom', 'field')), may hold values from 0 to 255, as said below
- tile_atm: int32 [2048], P(('dom', 'field')), may hold values from 0 to 255, as said below
- atm_owner: int32 [256], replicated, may hold values from 0 to 255, as said below
Outputs:
- atmosphere: float32 [30, 32768], P('field', 'dom')
Inputs may be any that keep to these rules, and one draw needn't show every extreme that they name: `neighbours`: the stencil of a block of partition p holds blocks of p, the last 2 blocks of partition p - 1 or the first 2 blocks of partition p + 1 (partitions are the aligned runs of 16 blocks; no wrap). `tile_src`: tile t names a block of partition t // 128, the partition that holds the tile. `tile_atm`: of the aligned runs of 64 tiles, no run has more than 16 tiles whose atmosphere tile has owner position in one aligned run of 16; in every draw each run reaches 16 for some owner. `atm_owner`: A permutation of the atmosphere tiles.
All inputs are finite; a program needn't handle non-finite values.
Results may differ from a plain program's by a relative error of at most 0.0042.
Values may be sent and summed in bfloat16 or wider, within the bound.
No kernel may reach another device: no remote copies, remote signals or barrier semaphores. Data moves between devices by JAX's collectives and lax.ppermute only.
A program may use at most 64 MiB of HBM per device.

v0:
```python
import jax
import jax.numpy as jnp
from jax import lax
from jax.sharding import PartitionSpec as P


def padded_2(shard, sides, width):
    for axis, dim in sides:
        size, length = (lax.axis_size(axis), shard.shape[dim])
        up = [(i, (i + 1) % size) for i in range(size - 1)]
        down = [(j, i) for i, j in up]
        last = lax.slice_in_dim(shard, length - width, length, axis=dim)
        initial = lax.slice_in_dim(shard, 0, width, axis=dim)
        before = lax.ppermute(last, axis, up)
        after = lax.ppermute(initial, axis, down)
        shard = jnp.concatenate([before, shard, after], axis=dim)
    return shard


def deliver(contribution, target_dev, local_slot, devices, capacity, owned):
    tile_count = target_dev.shape[0]
    tile_order = jnp.arange(tile_count, dtype=jnp.int32)
    before = jnp.sum(
        (
            (target_dev[:, None] == target_dev[None, :])
            & (tile_order[None, :] < tile_order[:, None])
        ).astype(jnp.int32),
        axis=1,
    )
    position = target_dev * capacity + before
    slot_count = devices * capacity
    matches = position[None, :] == jnp.arange(slot_count, dtype=jnp.int32)[:, None]
    chosen = jnp.sum(jnp.where(matches, tile_order[None, :], 0), axis=1)
    filled = jnp.any(matches, axis=1)
    outgoing = jnp.where(filled[:, None, None], contribution[chosen], 0.0)
    targets = jnp.where(filled, local_slot[chosen], -1)
    incoming, in_targets = (
        lax.all_to_all(outgoing, "dom", split_axis=0, concat_axis=0, tiled=True),
        lax.all_to_all(targets, "dom", split_axis=0, concat_axis=0, tiled=True),
    )
    selector = (in_targets[None, :] == jnp.arange(owned, dtype=jnp.int32)[:, None]).astype(
        jnp.float32
    )
    summed = jnp.einsum("ak,kfc->fac", selector, incoming, precision=lax.Precision.HIGHEST)
    return summed.reshape(summed.shape[0], owned * summed.shape[2])


def local(ocean, grad_weight, neighbours, remap_weight, tile_src, tile_atm, atm_owner):
    block_len = grad_weight.shape[2]
    field_rows = ocean.shape[0]
    nblocks = grad_weight.shape[0]
    device = lax.axis_index("dom")
    devices = lax.axis_size("dom")
    per_core = tile_atm.shape[0]
    capacity_base = max(2, 4 * per_core // devices)
    padded = padded_2(ocean, (("dom", 1),), nblocks * block_len)
    first_block = device * nblocks - nblocks
    extended = padded.reshape(field_rows, -1, block_len)
    local_ids = neighbours - first_block
    picked = jnp.take(extended, local_ids, axis=1)
    gradient = jnp.einsum(
        "fbkj,bkjo->fbo", picked, grad_weight, preferred_element_type=jnp.float32
    ).astype(jnp.bfloat16)
    source = jnp.concatenate([ocean.reshape(field_rows, nblocks, block_len), gradient], axis=2)
    source = lax.all_gather(source, "field", axis=0, tiled=True)
    local_src = tile_src - device * nblocks
    source_rows = jnp.take(source, local_src, axis=1)
    contribution = jnp.einsum(
        "ftj,tjc->tfc", source_rows, remap_weight, preferred_element_type=jnp.float32
    )
    atm_tiles = atm_owner.shape[0]
    atm_slot = jnp.sum(
        jnp.where(
            tile_atm[:, None] == jnp.arange(atm_tiles, dtype=jnp.int32)[None, :],
            atm_owner[None, :],
            0,
        ),
        axis=1,
    )
    owned = atm_tiles // devices
    target_dev = atm_slot // owned
    local_slot = atm_slot % owned
    summed = deliver(contribution, target_dev, local_slot, devices, capacity_base, owned)
    return lax.psum_scatter(summed, "field", scatter_dimension=0, tiled=True)


def solution(mesh):
    in_specs = (
        P("field", "dom"),
        P("dom", None, None, None),
        P("dom", None),
        P(("dom", "field"), None, None),
        P(("dom", "field")),
        P(("dom", "field")),
        P(),
    )
    out_specs = P("field", "dom")
    return jax.shard_map(local, mesh=mesh, in_specs=in_specs, out_specs=out_specs, check_vma=False)
```

profile of v0, /device:TPU:15, one launch (start us, length us, event | category | flops | bytes accessed | tf_op | source)
XLA Modules:
  0.0 153.9 jit_solution(14185718574713229053)
XLA Ops:
  0.0 3.1 %collective-permute-start = (bf16[15,2048]{1,0:T(8,128)(2,1)}, bf16[15,2048]{1,0:T(8,128)(2,1)S(1)}, u32[]{:S(2)}, u32[]{:S(2)}) collective-permute-start(bf16[15,2048]{1,0:T(8,128)(2,1)} %param.7), channel_id=1, source_target_pairs={{0,2},{2,4},{4,6},{6,8},{8,10},{10,12},{12,14},{14,16},{16,18},{18... | collective-permute-start | bytes 184328 | tf_op jit(solution)/shard_map/ppermute | solution.py:14
  3.1 2.2 %collective-permute-start.1 = (bf16[15,2048]{1,0:T(8,128)(2,1)}, bf16[15,2048]{1,0:T(8,128)(2,1)S(1)}, u32[]{:S(2)}, u32[]{:S(2)}) collective-permute-start(bf16[15,2048]{1,0:T(8,128)(2,1)} %param.7), channel_id=1, source_target_pairs={{2,0},{4,2},{6,4},{8,6},{10,8},{12,10},{14,12},{16,14},{18,16},{20... | collective-permute-start | bytes 184328 | tf_op jit(solution)/shard_map/ppermute | solution.py:15
  5.3 0.9 select_reduce_fusion.1
  6.2 0.2 convert_reduce_fusion
  6.4 0.1 fusion.17
  6.5 0.1 select_reduce_fusion
  6.6 1.9 %gather_fusion.3 = s32[256]{0:T(256)S(1)} fusion(s32[64]{0:T(128)S(1)} %get-tuple-element.9, s32[1024]{0:T(1024)S(1)} %pad_clamp_fusion), kind=kCustom, calls=%fused_computation.3 | custom fusion | bytes 3072 | tf_op jit(solution)/shard_map/gather | solution.py:36
  8.5 0.7 select_n.88
  9.2 6.6 %all-to-all-start.1 = ((s32[16,16,1]{1,2,0:T(1,128)}), s32[16,16,1]{1,2,0:T(1,128)S(1)}, u32[]{:S(2)}, u32[]{:S(2)}) async-start(s32[16,16,1]{1,2,0:T(1,128)} %bitcast.8), calls=%async_computation.1 | async-start | bytes 16384 | tf_op jit(solution)/shard_map/all_to_all | solution.py:39
  15.7 0.7 compare_and_fusion.1
  16.4 0.7 compare_and_fusion
  17.1 0.1 copy.40
  17.2 0.1 copy.41
  17.3 0.1 reshape.103
  17.4 0.9 copy.49
  18.3 0.0 collective-permute-done
  18.3 0.0 collective-permute-done.1
  18.3 0.9 pad_maximum_fusion
  19.2 0.1 copy.42
  19.3 0.6 gather_fusion
  19.9 2.9 %fusion.11 = bf16[15,16,256]{2,0,1:T(8,128)(2,1)S(1)} fusion(bf16[16,4,128,256]{3,2,1,0:T(8,128)(2,1)} %param.8, bf16[16,4,15,128]{3,2,1,0:T(8,128)(2,1)S(1)} %bitcast.41, pred[16,4]{1,0:T(8,128)(4,1)S(1)} %copy.40), kind=kOutput, calls=%fused_computation.14 | convolution fusion | flops 63098880 | bytes 4563008 | tf_op jit(solution)/shard_map/fbkj,bkjo->fbo/dot_general | solution.py:61
  22.9 3.5 %all_gather.3 = bf16[30,16,384]{2,1,0:T(8,128)(2,1)S(1)} all-gather(bf16[15,16,384]{2,1,0:T(8,128)(2,1)S(1)} %copy.44), channel_id=1, replica_groups=mesh['dom'=16,'field'=2] {'field'}, dimensions={0}, use_global_device_ids=true | all-gather | bytes 552960 | tf_op jit(solution)/shard_map/all_gather | solution.py:65
  26.4 0.1 copy.45
  26.5 0.9 gather_fusion.1
  27.4 4.0 %fusion.3 = f32[64,30,128]{2,1,0:T(8,128)S(1)} fusion(bf16[64,384,128]{2,1,0:T(8,128)(2,1)} %param.10, bf16[64,30,384]{2,1,0:T(8,128)(2,1)S(1)} %gather_fusion.1, pred[64]{0:T(512)(128)(4,1)S(1)} %get-tuple-element.5), kind=kOutput, calls=%fused_computation.7 | convolution fusion | flops 189480960 | bytes 8749120 | tf_op jit(solution)/shard_map/ftj,tjc->tfc/dot_general | solution.py:68
  31.4 3.0 %gather_fusion.2 = f32[256,30,128]{2,1,0:T(8,128)} fusion(f32[64,30,128]{2,1,0:T(8,128)S(1)} %fusion.3, s32[1024]{0:T(1024)S(1)} %pad_clamp_fusion), kind=kCustom, calls=%fused_computation.2 | custom fusion | bytes 7865344 | tf_op jit(solution)/shard_map/gather | solution.py:35
  34.4 4.0 %broadcast_select_fusion = f32[256,30,128]{2,1,0:T(8,128)} fusion(f32[256,30,128]{2,1,0:T(8,128)} %gather_fusion.2, pred[256]{0:T(512)(128)(4,1)S(1)} %fusion.17), kind=kLoop, calls=%fused_computation.6 | loop fusion | flops 983040 | bytes 7864576 | tf_op jit(solution)/shard_map/jit(_where)/select_n | solution.py:35
  38.4 0.0 all-to-all-done.1
  38.4 6.4 %all-to-all-start = ((f32[256,30,128]{2,1,0:T(8,128)}), f32[256,30,128]{2,1,0:T(8,128)}, u32[]{:S(2)}, u32[]{:S(2)}) async-start(f32[256,30,128]{2,1,0:T(8,128)} %broadcast_select_fusion), calls=%async_computation | async-start | bytes 8388608 | tf_op jit(solution)/shard_map/all_to_all | solution.py:38
  44.8 0.0 copy-start
  44.8 0.5 broadcast.180
  45.3 0.7 reduce.3
  46.0 0.1 eq.65
  46.1 93.8 %all-to-all-done = f32[256,30,128]{2,1,0:T(8,128)} async-done(((f32[256,30,128]{2,1,0:T(8,128)}), f32[256,30,128]{2,1,0:T(8,128)}, u32[]{:S(2)}, u32[]{:S(2)}) %all-to-all-start) | async-done | bytes 3932192 | tf_op jit(solution)/shard_map/all_to_all | solution.py:38
  139.9 5.6 %fusion.7 = f32[30,16,128]{2,1,0:T(8,128)S(1)} fusion(f32[256,30,128]{2,1,0:T(8,128)} %all-to-all-done, s32[256]{0:T(256)S(1)} %eq.65), kind=kOutput, calls=%fused_computation.12 | convolution fusion | flops 188747776 | bytes 4178944 | tf_op jit(solution)/shard_map/ak,kfc->fac/dot_general | solution.py:44
  145.5 0.1 copy.51
  145.6 4.3 %fusion = f32[16,2048]{1,0:T(8,128)S(1)} fusion(f32[30,2048]{1,0:T(8,128)S(1)} %bitcast.40), kind=kCustom, calls=%all-reduce-scatter | all-reduce-scatter fusion | flops 65537 | bytes 377344
  150.0 1.3 collective-permute-start.2
  151.3 0.0 copy-done
  151.3 0.6 dynamic-slice.4
  152.5 0.5 collective-permute-done.2
  153.0 0.2 concatenate.8
  153.2 0.7 constant_dynamic-slice_fusion
  (15 shorter events, 0.2 us)
Async XLA Ops:
  0.0 18.3 %collective-permute-start = (bf16[15,2048]{1,0:T(8,128)(2,1)}, bf16[15,2048]{1,0:T(8,128)(2,1)S(1)}, u32[]{:S(2)}, u32[]{:S(2)}) collective-permute-start(bf16[15,2048]{1,0:T(8,128)(2,1)} %param.7), channel_id=1, source_target_pairs={{0,2},{2,4},{4,6},{6,8},{8,10},{10,12},{12,14},{14,16},{16,18},{18... | collective-permute-start | bytes 184328 | tf_op jit(solution)/shard_map/ppermute | solution.py:14
  3.1 15.2 %collective-permute-start.1 = (bf16[15,2048]{1,0:T(8,128)(2,1)}, bf16[15,2048]{1,0:T(8,128)(2,1)S(1)}, u32[]{:S(2)}, u32[]{:S(2)}) collective-permute-start(bf16[15,2048]{1,0:T(8,128)(2,1)} %param.7), channel_id=1, source_target_pairs={{2,0},{4,2},{6,4},{8,6},{10,8},{12,10},{14,12},{16,14},{18,16},{20... | collective-permute-start | bytes 184328 | tf_op jit(solution)/shard_map/ppermute | solution.py:15
  9.2 29.3 %all-to-all-start.1 = ((s32[16,16,1]{1,2,0:T(1,128)}), s32[16,16,1]{1,2,0:T(1,128)S(1)}, u32[]{:S(2)}, u32[]{:S(2)}) async-start(s32[16,16,1]{1,2,0:T(1,128)} %bitcast.8), calls=%async_computation.1 | async-start | bytes 16384 | tf_op jit(solution)/shard_map/all_to_all | solution.py:39
  38.4 101.5 %all-to-all-start = ((f32[256,30,128]{2,1,0:T(8,128)}), f32[256,30,128]{2,1,0:T(8,128)}, u32[]{:S(2)}, u32[]{:S(2)}) async-start(f32[256,30,128]{2,1,0:T(8,128)} %broadcast_select_fusion), calls=%async_computation | async-start | bytes 8388608 | tf_op jit(solution)/shard_map/all_to_all | solution.py:38
  44.8 106.5 %copy-start = (u32[32]{0:T(128)S(1)}, u32[32]{0:T(128)}, u32[]{:S(2)}) copy-start(u32[32]{0:T(128)} %constant.76) | copy-start | bytes 388
  150.0 3.1 %collective-permute-start.2 = (f32[1,2048]{1,0:T(1,128)S(1)}, f32[1,2048]{1,0:T(1,128)S(1)}, u32[]{:S(2)}, u32[]{:S(2)}) collective-permute-start(f32[1,2048]{1,0:T(1,128)S(1)} %slice.8), channel_id=1, source_target_pairs={{0,1},{2,3},{4,5},{6,7},{8,9},{10,11},{12,13},{14,15},{16,17},{18,... | collective-permute-start | bytes 24584
where the time goes:
time: 154 us
  waiting for transfers between devices  94.4 us (61%)
  starting transfers between devices  19.5 us (13%)
  matrix products  12.5 us (8%)
  local copies, waits for them, and re-layouts  10.6 us (7%)
  other arithmetic  8.22 us (5%)
  blocking collectives  7.79 us (5%)
    all_to_all x1, waiting for transfers between devices, deliver(): lax.all_to_all(outgoing, 'dom', split_axis=0, concat_axis=0, tiled=True)  93.8 us
    all_to_all x1, starting transfers between devices, deliver(): lax.all_to_all(targets, 'dom', split_axis=0, concat_axis=0, tiled=True)  6.58 us
    all_to_all x1, starting transfers between devices, deliver(): lax.all_to_all(outgoing, 'dom', split_axis=0, concat_axis=0, tiled=True)  6.36 us
    dot_general x1, matrix products, deliver(): jnp.einsum('ak,kfc->fac', selector, incoming, precision=lax.Precision.HIG...  5.6 us
    unnamed x1, blocking collectives  4.29 us
    dot_general x1, matrix products, local(): jnp.einsum('ftj,tjc->tfc', source_rows, remap_weight, preferred_element_t...  4.05 us
    select_n x2, other arithmetic, deliver(): outgoing = jnp.where(filled[:, None, None], contribution[chosen], 0.0)  4.03 us
    all_gather x1, blocking collectives, local(): source = lax.all_gather(source, 'field', axis=0, tiled=True)  3.5 us
  transfers between devices with their start and end apart: 5, of which 2 were waited for; matrix products, arithmetic and copies ran while one was open for 16% of the time, Pallas kernels for 0%

commit v1 on v0

v1 whole, which is shorter than its diff:
```python
import functools

import jax
import jax.numpy as jnp
from jax import lax
from jax.experimental import pallas as pl
from jax.experimental.pallas import tpu as pltpu
from jax.sharding import PartitionSpec as P

HALO = 2
ROWS = 16

VMEM = pl.BlockSpec(memory_space=pltpu.VMEM)
SMEM = pl.BlockSpec(memory_space=pltpu.SMEM)
HBM = pl.BlockSpec(memory_space=pltpu.HBM)


def contribute(
    nb_s, src_s, own, other, bef_own, bef_other, aft_own, aft_other, gw_any, rw_any,
    keep, send, xs, source, gw, rw, gsem, rsem,
):
    nblk, nk, blk, _ = gw_any.shape
    tiles = rw_any.shape[0]
    fields = own.shape[0]
    gchunks, rchunks = gsem.shape[0], rsem.shape[0]
    gper, rper = nblk // gchunks, tiles // rchunks

    def gcopy(i):
        return pltpu.make_async_copy(
            gw_any.at[pl.ds(i * gper, gper)], gw.at[pl.ds(i * gper, gper)], gsem.at[i]
        )

    def rcopy(i):
        return pltpu.make_async_copy(
            rw_any.at[pl.ds(i * rper, rper)], rw.at[pl.ds(i * rper, rper)], rsem.at[i]
        )

    for i in range(gchunks):
        gcopy(i).start()
    for i in range(rchunks):
        rcopy(i).start()

    xs[...] = jnp.zeros_like(xs)
    for group, (mid, before, after) in enumerate(
        ((own, bef_own, aft_own), (other, bef_other, aft_other))
    ):
        rows = pl.ds(group * ROWS, fields)
        for h in range(HALO):
            cols = pl.ds(h * blk, blk)
            xs[h, rows, :] = before[:, cols]
            xs[HALO + nblk + h, rows, :] = after[:, cols]
        for b in range(nblk):
            xs[HALO + b, rows, :] = mid[:, pl.ds(b * blk, blk)]

    first = lax.axis_index("dom") * nblk
    for b in range(nblk):
        if b % gper == 0:
            gcopy(b // gper).wait()
        picked = [xs[nb_s[k, b] - first + HALO] for k in range(nk)]
        grad = jnp.dot(
            jnp.concatenate(picked, axis=1),
            gw[b].reshape(nk * blk, 2 * blk),
            preferred_element_type=jnp.float32,
        )
        source[b, :, pl.ds(0, blk)] = xs[HALO + b]
        source[b, :, pl.ds(blk, 2 * blk)] = grad.astype(source.dtype)

    def tile_chunk(i, carry):
        rcopy(i).wait()
        for j in range(rper):
            t = i * rper + j
            out = jnp.dot(
                source[src_s[t] - first], rw[t], preferred_element_type=jnp.float32
            )
            keep[t] = out[:ROWS]
            send[t] = out[ROWS:].astype(send.dtype)
        return carry

    lax.fori_loop(0, rchunks, tile_chunk, 0)


def gather_slots(atm_s, atm_other_s, owner_s, keep, recv, dense, acc):
    tiles = keep.shape[0]
    dests, fields, owned, _ = dense.shape
    acc[...] = jnp.zeros_like(acc)

    def add(t, carry):
        a = owner_s[atm_s[t]]
        acc[pl.ds(pl.multiple_of(a * ROWS, ROWS), ROWS), :] += keep[t]
        b = owner_s[atm_other_s[t]]
        acc[pl.ds(pl.multiple_of(b * ROWS, ROWS), ROWS), :] += recv[t].astype(jnp.float32)
        return carry

    lax.fori_loop(0, tiles, add, 0, unroll=4)

    def write(d, carry):
        for f in range(fields):
            rows = acc[pl.ds(d * (owned * ROWS) + f, owned, stride=ROWS), :]
            dense[d, f] = rows.astype(dense.dtype)
        return carry

    lax.fori_loop(0, dests, write, 0)


def total(parts, out, acc):
    srcs, fields, owned, width = parts.shape
    for f in range(fields):
        value = parts[0, f].astype(jnp.float32)
        for s in range(1, srcs):
            value = value + parts[s, f].astype(jnp.float32)
        acc[pl.ds(f * owned, owned), :] = value
    for a in range(owned):
        out[:, pl.ds(a * width, width)] = acc[pl.ds(a, fields, stride=owned), :]


def local(ocean, grad_weight, neighbours, remap_weight, tile_src, tile_atm, atm_owner):
    fields = ocean.shape[0]
    nblk, nk, blk, _ = grad_weight.shape
    tiles, depth, acell = remap_weight.shape
    devices = lax.axis_size("dom")
    owned = atm_owner.shape[0] // devices
    width = HALO * blk
    swap = [(0, 1), (1, 0)]

    up, down, up_x, down_x = [], [], [], []
    for i in range(devices - 1):
        for f in range(2):
            up.append((2 * i + f, 2 * i + 2 + f))
            down.append((2 * i + 2 + f, 2 * i + f))
            up_x.append((2 * i + f, 2 * i + 3 - f))
            down_x.append((2 * i + 2 + f, 2 * i + 1 - f))
    both = ("dom", "field")
    last, initial = ocean[:, -width:], ocean[:, :width]
    bef_own = lax.ppermute(last, both, up)
    aft_own = lax.ppermute(initial, both, down)
    bef_other = lax.ppermute(last, both, up_x)
    aft_other = lax.ppermute(initial, both, down_x)
    other = lax.ppermute(ocean, "field", swap)
    atm_other = lax.ppermute(tile_atm, "field", swap)

    gchunks, rchunks = min(8, nblk), min(8, tiles)
    keep, send = pl.pallas_call(
        contribute,
        out_shape=(
            jax.ShapeDtypeStruct((tiles, ROWS, acell), jnp.float32),
            jax.ShapeDtypeStruct((tiles, ROWS, acell), jnp.bfloat16),
        ),
        in_specs=[SMEM] * 2 + [VMEM] * 6 + [HBM] * 2,
        out_specs=(VMEM, VMEM),
        scratch_shapes=[
            pltpu.VMEM((nblk + 2 * HALO, 2 * ROWS, blk), jnp.bfloat16),
            pltpu.VMEM((nblk, 2 * ROWS, depth), jnp.bfloat16),
            pltpu.VMEM(grad_weight.shape, jnp.bfloat16),
            pltpu.VMEM(remap_weight.shape, jnp.bfloat16),
            pltpu.SemaphoreType.DMA((gchunks,)),
            pltpu.SemaphoreType.DMA((rchunks,)),
        ],
        compiler_params=pltpu.CompilerParams(vmem_limit_bytes=24 << 20),
        cost_estimate=pl.CostEstimate(
            flops=2 * 30 * (grad_weight.size + remap_weight.size),
            bytes_accessed=2 * (grad_weight.size + remap_weight.size),
            transcendentals=0,
        ),
        name="contribute",
    )(
        neighbours.T, tile_src, ocean, other, bef_own, bef_other, aft_own, aft_other,
        grad_weight, remap_weight,
    )
    recv = lax.ppermute(send, "field", swap)
    slots = devices * owned
    dense = pl.pallas_call(
        gather_slots,
        out_shape=jax.ShapeDtypeStruct((devices, fields, owned, acell), jnp.bfloat16),
        in_specs=[SMEM] * 3 + [VMEM] * 2,
        out_specs=VMEM,
        scratch_shapes=[pltpu.VMEM((slots * ROWS, acell), jnp.float32)],
        compiler_params=pltpu.CompilerParams(vmem_limit_bytes=40 << 20),
        name="gather_slots",
    )(tile_atm, atm_other, atm_owner, keep, recv)
    parts = lax.all_to_all(dense, "dom", split_axis=0, concat_axis=0, tiled=True)
    return pl.pallas_call(
        total,
        out_shape=jax.ShapeDtypeStruct((fields, owned * acell), jnp.float32),
        in_specs=[VMEM],
        out_specs=VMEM,
        scratch_shapes=[pltpu.VMEM((fields * owned, acell), jnp.float32)],
        compiler_params=pltpu.CompilerParams(vmem_limit_bytes=40 << 20),
        name="total",
    )(parts)


def solution(mesh):
    in_specs = (
        P("field", "dom"),
        P("dom", None, None, None),
        P("dom", None),
        P(("dom", "field"), None, None),
        P(("dom", "field")),
        P(("dom", "field")),
        P(),
    )
    out_specs = P("field", "dom")
    return jax.shard_map(local, mesh=mesh, in_specs=in_specs, out_specs=out_specs, check_vma=False)
```

time: 154 us -> 66.3 us (0.43)
  the two profiles are of different devices: /device:TPU:15 before, /device:TPU:0 now
where the time goes in v1:
time: 66.3 us; the launch traced here: 65.9 us
  blocking collectives  33.8 us (51%)
  starting transfers between devices  13.9 us (21%)
  local copies, waits for them, and re-layouts  7.87 us (12%)
  Pallas kernels  7.82 us (12%)
  waiting for transfers between devices  2.35 us (4%)
    all_to_all x1, blocking collectives, local(): lax.all_to_all(dense, 'dom', split_axis=0, concat_axis=0, tiled=True)  33.8 us
    unnamed x14, local copies, waits for them, and re-layouts  7.15 us
    ppermute x1, starting transfers between devices, local(): bef_other = lax.ppermute(last, both, up_x)  5.75 us
    pallas_call x1, Pallas kernels, local(): pl.pallas_call(contribute, out_shape=(jax.ShapeDtypeStruct((tiles, ROWS,...  5.22 us
    ppermute x1, starting transfers between devices, local(): bef_own = lax.ppermute(last, both, up)  4.54 us
    pallas_call x1, Pallas kernels, local(): pl.pallas_call(gather_slots, out_shape=jax.ShapeDtypeStruct((devices, fie...  1.79 us
  transfers between devices with their start and end apart: 7, of which 2 were waited for; matrix products, arithmetic and copies ran while one was open for 1% of the time, Pallas kernels for 0%

profile of v1, /device:TPU:0, one launch (start us, length us, event | category | flops | bytes accessed | tf_op | source)
XLA Modules:
  0.0 65.9 jit_solution(7644117525157746755)
XLA Ops:
  0.0 0.0 copy-start.6
  0.0 0.0 copy-start.4
  0.0 0.5 collective-permute-start.1
  0.5 0.7 %fusion = (bf16[15,256]{1,0:T(8,128)(2,1)S(1)}, bf16[15,256]{1,0:T(8,128)(2,1)S(1)}) fusion(bf16[15,2048]{1,0:T(8,128)(2,1)} %own.1), kind=kLoop, calls=%fused_computation | loop fusion | bytes 30720 | tf_op jit(solution)/shard_map/slice | solution.py:133
  1.2 1.3 %collective-permute-start.5 = (bf16[15,256]{1,0:T(8,128)(2,1)S(1)}, bf16[15,256]{1,0:T(8,128)(2,1)S(1)}, u32[]{:S(2)}, u32[]{:S(2)}) collective-permute-start(bf16[15,256]{1,0:T(8,128)(2,1)S(1)} %get-tuple-element.9), channel_id=1, source_target_pairs={{2,1},{3,0},{4,3},{5,2},{6,5},{7,4},{8,7},{9,6},{10,9},{11,8},{12,... | collective-permute-start | bytes 23048 | tf_op jit(solution)/shard_map/ppermute | solution.py:137
  2.5 1.3 %collective-permute-start.4 = (bf16[15,256]{1,0:T(8,128)(2,1)S(1)}, bf16[15,256]{1,0:T(8,128)(2,1)S(1)}, u32[]{:S(2)}, u32[]{:S(2)}) collective-permute-start(bf16[15,256]{1,0:T(8,128)(2,1)S(1)} %get-tuple-element.9), channel_id=1, source_target_pairs={{2,0},{3,1},{4,2},{5,3},{6,4},{7,5},{8,6},{9,7},{10,8},{11,9},{12,... | collective-permute-start | bytes 23048 | tf_op jit(solution)/shard_map/ppermute | solution.py:135
  3.8 5.8 %collective-permute-start.3 = (bf16[15,256]{1,0:T(8,128)(2,1)S(1)}, bf16[15,256]{1,0:T(8,128)(2,1)S(1)}, u32[]{:S(2)}, u32[]{:S(2)}) collective-permute-start(bf16[15,256]{1,0:T(8,128)(2,1)S(1)} %get-tuple-element.10), channel_id=1, source_target_pairs={{0,3},{1,2},{2,5},{3,4},{4,7},{5,6},{6,9},{7,8},{8,11},{9,10},{10,... | collective-permute-start | bytes 23048 | tf_op jit(solution)/shard_map/ppermute | solution.py:136
  9.6 4.5 %collective-permute-start.2 = (bf16[15,256]{1,0:T(8,128)(2,1)S(1)}, bf16[15,256]{1,0:T(8,128)(2,1)S(1)}, u32[]{:S(2)}, u32[]{:S(2)}) collective-permute-start(bf16[15,256]{1,0:T(8,128)(2,1)S(1)} %get-tuple-element.10), channel_id=1, source_target_pairs={{0,2},{1,3},{2,4},{3,5},{4,6},{5,7},{6,8},{7,9},{8,10},{9,11},{10,... | collective-permute-start | bytes 23048 | tf_op jit(solution)/shard_map/ppermute | solution.py:134
  14.1 0.0 collective-permute-done.5.aft_other
  14.1 0.0 collective-permute-done.4.aft_own
  14.1 0.0 collective-permute-done.3.bef_other
  14.1 1.3 %collective-permute-done.2.bef_own = bf16[15,256]{1,0:T(8,128)(2,1)S(1)} collective-permute-done((bf16[15,256]{1,0:T(8,128)(2,1)S(1)}, bf16[15,256]{1,0:T(8,128)(2,1)S(1)}, u32[]{:S(2)}, u32[]{:S(2)}) %collective-permute-start.2) | collective-permute-done | bytes 7712 | tf_op jit(solution)/shard_map/ppermute | solution.py:134
  15.5 0.0 collective-permute-done.1.other
  15.5 0.0 copy-start
  15.5 2.8 %copy-done = bf16[64,384,128]{2,1,0:T(8,128)(2,1)S(1)} copy-done((bf16[64,384,128]{2,1,0:T(8,128)(2,1)S(1)}, bf16[64,384,128]{2,1,0:T(8,128)(2,1)}, u32[]{:S(2)}) %copy-start) | copy-done | bytes 6291480
  18.2 0.0 copy-start.1
  18.2 2.2 %copy-done.1 = bf16[16,4,128,256]{3,2,1,0:T(8,128)(2,1)S(1)} copy-done((bf16[16,4,128,256]{3,2,1,0:T(8,128)(2,1)S(1)}, bf16[16,4,128,256]{3,2,1,0:T(8,128)(2,1)}, u32[]{:S(2)}) %copy-start.1) | copy-done | bytes 4194328
  20.4 0.0 copy-start.2
  20.4 0.8 %copy-done.2 = bf16[15,2048]{1,0:T(8,128)(2,1)S(1)} copy-done((bf16[15,2048]{1,0:T(8,128)(2,1)S(1)}, bf16[15,2048]{1,0:T(8,128)(2,1)}, u32[]{:S(2)}) %copy-start.2) | copy-done | bytes 61464
  21.3 0.0 copy-start.3
  21.3 0.7 %copy-done.3 = s32[16,4]{0,1:T(4,128)S(1)} copy-done((s32[16,4]{0,1:T(4,128)S(1)}, s32[16,4]{0,1:T(4,128)}, u32[]{:S(2)}) %copy-start.3) | copy-done | bytes 280
  22.0 0.0 copy-start.5
  22.0 0.7 copy-done.5
  22.6 5.2 %contribute.1 = (f32[64,16,128]{2,1,0:T(8,128)S(1)}, bf16[64,16,128]{2,1,0:T(8,128)(2,1)S(1)}) custom-call(s32[4,16]{1,0:T(4,128)S(1)} %bitcast.1, s32[64]{0:T(128)S(1)} %copy-done.5, bf16[15,2048]{1,0:T(8,128)(2,1)S(1)} %copy-done.2, bf16[15,2048]{1,0:T(8,128)(2,1)S(1)} %collective-permute-done.1.other, bf16[15,256]{1,0:T(8,128)(2,1)S(1)} %collective-permute-done.2.bef_own, ...), custom_call_target="tpu_custom_call" | custom-call | flops 314572800 | bytes 10485760 | tf_op jit(solution)/shard_map/contribute/pallas_call | solution.py:142
  27.8 0.1 collective-permute-start.6
  27.9 0.0 copy-done.6
  27.9 0.5 collective-permute-start
  28.4 1.0 %collective-permute-done.atm_other_s = s32[64]{0:T(128)S(1)} collective-permute-done((s32[64]{0:T(128)S(1)}, s32[64]{0:T(128)S(1)}, u32[]{:S(2)}, u32[]{:S(2)}) %collective-permute-start) | collective-permute-done | bytes 288 | tf_op jit(solution)/shard_map/ppermute | solution.py:139
  29.4 0.0 collective-permute-done.6.recv
  29.4 0.0 copy-done.4
  29.4 1.8 %gather_slots.1 = bf16[16,15,16,128]{3,2,1,0:T(8,128)(2,1)S(1)} custom-call(s32[64]{0:T(128)S(1)} %copy-done.6, s32[64]{0:T(128)S(1)} %collective-permute-done.atm_other_s, s32[256]{0:T(256)S(1)} %copy-done.4, f32[64,16,128]{2,1,0:T(8,128)S(1)} %get-tuple-element.7.keep, bf16[64,16,128]{2,1,0:T(8,128)(2,1)S(1)} %collective-permute-done.6.recv), custom_call_target="tpu_custom_call" | custom-call | tf_op jit(solution)/shard_map/gather_slots/pallas_call | solution.py:171
  31.2 33.8 %all_to_all.5.parts = bf16[16,15,16,128]{3,2,1,0:T(8,128)(2,1)S(1)} all-to-all(bf16[16,15,16,128]{3,2,1,0:T(8,128)(2,1)S(1)} %gather_slots.1), channel_id=1, replica_groups=mesh['dom'=16,'field'=2] {'dom'}, dimensions={0} | all-to-all | bytes 1966080 | tf_op jit(solution)/shard_map/all_to_all | solution.py:180
  65.1 0.8 %total.1 = f32[15,2048]{1,0:T(8,128)} custom-call(bf16[16,15,16,128]{3,2,1,0:T(8,128)(2,1)S(1)} %all_to_all.5.parts), custom_call_target="tpu_custom_call" | custom-call | tf_op jit(solution)/shard_map/total/pallas_call | solution.py:181
Async XLA Ops:
  0.0 27.9 %copy-start.6 = (s32[64]{0:T(128)S(1)}, s32[64]{0:T(128)}, u32[]{:S(2)}) copy-start(s32[64]{0:T(128)} %atm_s.1) | copy-start | bytes 772
  0.0 29.4 %copy-start.4 = (s32[256]{0:T(256)S(1)}, s32[256]{0:T(256)}, u32[]{:S(2)}) copy-start(s32[256]{0:T(256)} %owner_s.1) | copy-start | bytes 3076
  0.0 15.5 %collective-permute-start.1 = (bf16[15,2048]{1,0:T(8,128)(2,1)}, bf16[15,2048]{1,0:T(8,128)(2,1)S(1)}, u32[]{:S(2)}, u32[]{:S(2)}) collective-permute-start(bf16[15,2048]{1,0:T(8,128)(2,1)} %own.1), channel_id=1, source_target_pairs={{0,1},{1,0},{2,3},{3,2},{4,5},{5,4},{6,7},{7,6},{8,9},{9,8},{10,11... | collective-permute-start | bytes 184328 | tf_op jit(solution)/shard_map/ppermute | solution.py:138
  1.2 12.9 %collective-permute-start.5 = (bf16[15,256]{1,0:T(8,128)(2,1)S(1)}, bf16[15,256]{1,0:T(8,128)(2,1)S(1)}, u32[]{:S(2)}, u32[]{:S(2)}) collective-permute-start(bf16[15,256]{1,0:T(8,128)(2,1)S(1)} %get-tuple-element.9), channel_id=1, source_target_pairs={{2,1},{3,0},{4,3},{5,2},{6,5},{7,4},{8,7},{9,6},{10,9},{11,8},{12,... | collective-permute-start | bytes 23048 | tf_op jit(solution)/shard_map/ppermute | solution.py:137
  2.5 11.6 %collective-permute-start.4 = (bf16[15,256]{1,0:T(8,128)(2,1)S(1)}, bf16[15,256]{1,0:T(8,128)(2,1)S(1)}, u32[]{:S(2)}, u32[]{:S(2)}) collective-permute-start(bf16[15,256]{1,0:T(8,128)(2,1)S(1)} %get-tuple-element.9), channel_id=1, source_target_pairs={{2,0},{3,1},{4,2},{5,3},{6,4},{7,5},{8,6},{9,7},{10,8},{11,9},{12,... | collective-permute-start | bytes 23048 | tf_op jit(solution)/shard_map/ppermute | solution.py:135
  3.8 10.3 %collective-permute-start.3 = (bf16[15,256]{1,0:T(8,128)(2,1)S(1)}, bf16[15,256]{1,0:T(8,128)(2,1)S(1)}, u32[]{:S(2)}, u32[]{:S(2)}) collective-permute-start(bf16[15,256]{1,0:T(8,128)(2,1)S(1)} %get-tuple-element.10), channel_id=1, source_target_pairs={{0,3},{1,2},{2,5},{3,4},{4,7},{5,6},{6,9},{7,8},{8,11},{9,10},{10,... | collective-permute-start | bytes 23048 | tf_op jit(solution)/shard_map/ppermute | solution.py:136
  9.6 5.9 %collective-permute-start.2 = (bf16[15,256]{1,0:T(8,128)(2,1)S(1)}, bf16[15,256]{1,0:T(8,128)(2,1)S(1)}, u32[]{:S(2)}, u32[]{:S(2)}) collective-permute-start(bf16[15,256]{1,0:T(8,128)(2,1)S(1)} %get-tuple-element.10), channel_id=1, source_target_pairs={{0,2},{1,3},{2,4},{3,5},{4,6},{5,7},{6,8},{7,9},{8,10},{9,11},{10,... | collective-permute-start | bytes 23048 | tf_op jit(solution)/shard_map/ppermute | solution.py:134
  15.5 2.8 %copy-start = (bf16[64,384,128]{2,1,0:T(8,128)(2,1)S(1)}, bf16[64,384,128]{2,1,0:T(8,128)(2,1)}, u32[]{:S(2)}) copy-start(bf16[64,384,128]{2,1,0:T(8,128)(2,1)} %rw_any.1) | copy-start | bytes 18874372
  18.2 2.2 %copy-start.1 = (bf16[16,4,128,256]{3,2,1,0:T(8,128)(2,1)S(1)}, bf16[16,4,128,256]{3,2,1,0:T(8,128)(2,1)}, u32[]{:S(2)}) copy-start(bf16[16,4,128,256]{3,2,1,0:T(8,128)(2,1)} %gw_any.1) | copy-start | bytes 12582916
  20.4 0.8 %copy-start.2 = (bf16[15,2048]{1,0:T(8,128)(2,1)S(1)}, bf16[15,2048]{1,0:T(8,128)(2,1)}, u32[]{:S(2)}) copy-start(bf16[15,2048]{1,0:T(8,128)(2,1)} %own.1) | copy-start | bytes 184324
  21.3 0.7 %copy-start.3 = (s32[16,4]{0,1:T(4,128)S(1)}, s32[16,4]{0,1:T(4,128)}, u32[]{:S(2)}) copy-start(s32[16,4]{0,1:T(4,128)} %param.9) | copy-start | bytes 772
  22.0 0.7 copy-start.5
  27.8 1.6 %collective-permute-start.6 = (bf16[64,16,128]{2,1,0:T(8,128)(2,1)S(1)}, bf16[64,16,128]{2,1,0:T(8,128)(2,1)S(1)}, u32[]{:S(2)}, u32[]{:S(2)}) collective-permute-start(bf16[64,16,128]{2,1,0:T(8,128)(2,1)S(1)} %get-tuple-element.8), channel_id=1, source_target_pairs={{0,1},{1,0},{2,3},{3,2},{4,5},{5,4},{6,7},{7,6},{8,9},{9,8},{10,11... | collective-permute-start | bytes 786440 | tf_op jit(solution)/shard_map/ppermute | solution.py:169
  27.9 1.5 %collective-permute-start = (s32[64]{0:T(128)S(1)}, s32[64]{0:T(128)S(1)}, u32[]{:S(2)}, u32[]{:S(2)}) collective-permute-start(s32[64]{0:T(128)S(1)} %copy-done.6), channel_id=1, source_target_pairs={{0,1},{1,0},{2,3},{3,2},{4,5},{5,4},{6,7},{7,6},{8,9},{9,8},{10,11... | collective-permute-start | bytes 776 | tf_op jit(solution)/shard_map/ppermute | solution.py:139

commit v2 on v1

--- a/solution.py
+++ b/solution.py
@@ -15,8 +15,18 @@
 HBM = pl.BlockSpec(memory_space=pltpu.HBM)
 
 
+def in_hbm(x):
+    return pltpu.with_memory_space_constraint(x, pltpu.HBM)
+
+
+def stage(ocean, nb, src, own, nb_v, src_v):
+    own[...] = ocean[...]
+    nb_v[...] = nb[...]
+    src_v[...] = src[...]
+
+
 def contribute(
-    nb_s, src_s, own, other, bef_own, bef_other, aft_own, aft_other, gw_any, rw_any,
+    nb_s, src_s, own, other, near, far, atm_any, gw_any, rw_any,
     keep, send, xs, source, gw, rw, gsem, rsem,
 ):
     nblk, nk, blk, _ = gw_any.shape
@@ -40,15 +50,20 @@
     for i in range(rchunks):
         rcopy(i).start()
 
+    del atm_any
     xs[...] = jnp.zeros_like(xs)
-    for group, (mid, before, after) in enumerate(
-        ((own, bef_own, aft_own), (other, bef_other, aft_other))
-    ):
+    core = lax.axis_index("field")
+    odd = lax.axis_index("dom") % 2
+    near_is_after = odd == core
+    after, before = HALO + nblk, 0
+    near_at = jnp.where(near_is_after, after, before)
+    far_at = jnp.where(near_is_after, before, after)
+    for group, mid in enumerate((own, other)):
         rows = pl.ds(group * ROWS, fields)
         for h in range(HALO):
             cols = pl.ds(h * blk, blk)
-            xs[h, rows, :] = before[:, cols]
-            xs[HALO + nblk + h, rows, :] = after[:, cols]
+            xs[near_at + h, rows, :] = near[group, :, cols]
+            xs[far_at + h, rows, :] = far[1 - group, :, cols]
         for b in range(nblk):
             xs[HALO + b, rows, :] = mid[:, pl.ds(b * blk, blk)]
 
@@ -122,21 +137,35 @@
     width = HALO * blk
     swap = [(0, 1), (1, 0)]
 
-    up, down, up_x, down_x = [], [], [], []
-    for i in range(devices - 1):
-        for f in range(2):
-            up.append((2 * i + f, 2 * i + 2 + f))
-            down.append((2 * i + 2 + f, 2 * i + f))
-            up_x.append((2 * i + f, 2 * i + 3 - f))
-            down_x.append((2 * i + 2 + f, 2 * i + 1 - f))
-    both = ("dom", "field")
-    last, initial = ocean[:, -width:], ocean[:, :width]
-    bef_own = lax.ppermute(last, both, up)
-    aft_own = lax.ppermute(initial, both, down)
-    bef_other = lax.ppermute(last, both, up_x)
-    aft_other = lax.ppermute(initial, both, down_x)
+    pairs = []
+    for i in range(0, devices - 1, 2):
+        pairs += [(2 * i, 2 * i + 2), (2 * i + 2, 2 * i)]
+    for i in range(1, devices - 1, 2):
+        pairs += [(2 * i + 1, 2 * i + 3), (2 * i + 3, 2 * i + 1)]
+    odd = lax.axis_index("dom") % 2 == 1
+    core = lax.axis_index("field")
+    ends_up = odd == (core == 1)
+
     other = lax.ppermute(ocean, "field", swap)
     atm_other = lax.ppermute(tile_atm, "field", swap)
+    own, nb_v, src_v = pl.pallas_call(
+        stage,
+        out_shape=(
+            jax.ShapeDtypeStruct(ocean.shape, ocean.dtype),
+            jax.ShapeDtypeStruct((nk, nblk), jnp.int32),
+            jax.ShapeDtypeStruct(tile_src.shape, jnp.int32),
+        ),
+        in_specs=[VMEM] * 3,
+        out_specs=(VMEM,) * 3,
+        compiler_params=pltpu.CompilerParams(vmem_limit_bytes=24 << 20),
+        name="stage",
+    )(in_hbm(ocean), in_hbm(neighbours.T), in_hbm(tile_src))
+    ends = jnp.stack([
+        jnp.where(ends_up, own[:, -width:], own[:, :width]),
+        jnp.where(ends_up, other[:, -width:], other[:, :width]),
+    ])
+    near = lax.ppermute(ends, ("dom", "field"), pairs)
+    far = lax.ppermute(near, "field", swap)
 
     gchunks, rchunks = min(8, nblk), min(8, tiles)
     keep, send = pl.pallas_call(
@@ -145,7 +174,7 @@
             jax.ShapeDtypeStruct((tiles, ROWS, acell), jnp.float32),
             jax.ShapeDtypeStruct((tiles, ROWS, acell), jnp.bfloat16),
         ),
-        in_specs=[SMEM] * 2 + [VMEM] * 6 + [HBM] * 2,
+        in_specs=[SMEM] * 2 + [VMEM] * 4 + [HBM] * 3,
         out_specs=(VMEM, VMEM),
         scratch_shapes=[
             pltpu.VMEM((nblk + 2 * HALO, 2 * ROWS, blk), jnp.bfloat16),
@@ -163,8 +192,8 @@
         ),
         name="contribute",
     )(
-        neighbours.T, tile_src, ocean, other, bef_own, bef_other, aft_own, aft_other,
-        grad_weight, remap_weight,
+        nb_v, src_v, own, other, near, far, atm_other, in_hbm(grad_weight),
+        in_hbm(remap_weight),
     )
     recv = lax.ppermute(send, "field", swap)
     slots = devices * owned

time: 66.3 us -> 53.5 us (0.81)
  local copies, waits for them, and re-layouts: 7.87 us -> 0.01 us
  starting transfers between devices: 13.9 us -> 6.15 us
  Pallas kernels: 7.82 us -> 10.2 us
  waiting for transfers between devices: 2.35 us -> 4.08 us
  blocking collectives: 33.8 us -> 32.8 us
    ppermute x4 -> x2, starting transfers between devices: 12.9 us -> 4.74 us  [the longest x1 4.73 us: local(): near = lax.ppermute(ends, ('dom', 'field'), pairs)]
    unnamed x14 -> x4, local copies, waits for them, and re-layouts: 7.15 us -> 0.01 us
    pallas_call x1, Pallas kernels: 5.22 us -> 6.77 us  [local(): pl.pallas_call(contribute, out_shape=(jax.ShapeDtypeStruct((tiles, ROWS,...]
    ppermute x1, waiting for transfers between devices: 0.01 us -> 1.19 us  [local(): recv = lax.ppermute(send, 'field', swap)]
    all_to_all x1, blocking collectives: 33.8 us -> 32.8 us  [local(): lax.all_to_all(dense, 'dom', split_axis=0, concat_axis=0, tiled=True)]
    pallas_call x0 -> x1, Pallas kernels: none -> 0.87 us  [local(): pl.pallas_call(stage, out_shape=(jax.ShapeDtypeStruct(ocean.shape, ocean....]
    slice x1 -> x0, local copies, waits for them, and re-layouts: 0.72 us -> none  [local(): last, initial = (ocean[:, -width:], ocean[:, :width])]
    ppermute x4 -> x2, waiting for transfers between devices: 1.33 us -> 1.71 us  [the longest x1 1.7 us: local(): near = lax.ppermute(ends, ('dom', 'field'), pairs)]
  transfers between devices with their start and end apart: 7 -> 5, of which waited for: 2 -> 4; matrix products, arithmetic and copies ran while one was open for 1% -> 0% of each run, Pallas kernels for 0% -> 2%
where the time goes in v2:
time: 53.5 us; the launch traced here: 53.3 us
  blocking collectives  32.8 us (61%)
  Pallas kernels  10.2 us (19%)
  starting transfers between devices  6.15 us (11%)
  waiting for transfers between devices  4.08 us (8%)
    all_to_all x1, blocking collectives, local(): lax.all_to_all(dense, 'dom', split_axis=0, concat_axis=0, tiled=True)  32.8 us
    pallas_call x1, Pallas kernels, local(): pl.pallas_call(contribute, out_shape=(jax.ShapeDtypeStruct((tiles, ROWS,...  6.77 us
    ppermute x1, starting transfers between devices, local(): near = lax.ppermute(ends, ('dom', 'field'), pairs)  4.73 us
    pallas_call x1, Pallas kernels, local(): pl.pallas_call(gather_slots, out_shape=jax.ShapeDtypeStruct((devices, fie...  1.79 us
    ppermute x1, waiting for transfers between devices, local(): near = lax.ppermute(ends, ('dom', 'field'), pairs)  1.7 us
    ppermute x1, waiting for transfers between devices, local(): recv = lax.ppermute(send, 'field', swap)  1.19 us
  transfers between devices with their start and end apart: 5, of which 4 were waited for; matrix products, arithmetic and copies ran while one was open for 0% of the time, Pallas kernels for 2%

profile of v2, /device:TPU:0, one launch (start us, length us, event | category | flops | bytes accessed | tf_op | source)
XLA Modules:
  0.0 53.3 jit_solution(17601053138185727330)
XLA Ops:
  0.0 0.0 copy-start.1
  0.0 0.0 copy-start
  0.0 0.5 collective-permute-start.1
  0.5 0.9 %stage.1 = (bf16[15,2048]{1,0:T(8,128)(2,1)S(1)}, s32[4,16]{1,0:T(4,128)S(1)}, s32[64]{0:T(128)S(1)}) custom-call(bf16[15,2048]{1,0:T(8,128)(2,1)} %ocean.1, s32[4,16]{1,0:T(4,128)} %bitcast.5, s32[64]{0:T(128)} %src.1), custom_call_target="tpu_custom_call" | custom-call | tf_op jit(solution)/shard_map/stage/pallas_call | solution.py:151
  1.4 0.2 collective-permute-done.1.other
  1.6 4.7 %collective-permute-start.2 = (bf16[2,15,256]{2,1,0:T(8,128)(2,1)S(1)}, bf16[2,15,256]{2,1,0:T(8,128)(2,1)S(1)}, u32[]{:S(2)}, u32[]{:S(2)}) collective-permute-start(bf16[2,15,256]{2,1,0:T(8,128)(2,1)S(1)} %pad_maximum_fusion), channel_id=1, source_target_pairs={{0,2},{2,0},{4,6},{6,4},{8,10},{10,8},{12,14},{14,12},{16,18},{18,... | collective-permute-start | bytes 46088 | tf_op jit(solution)/shard_map/ppermute | solution.py:167
  6.4 1.7 %collective-permute-done.2.near = bf16[2,15,256]{2,1,0:T(8,128)(2,1)S(1)} collective-permute-done((bf16[2,15,256]{2,1,0:T(8,128)(2,1)S(1)}, bf16[2,15,256]{2,1,0:T(8,128)(2,1)S(1)}, u32[]{:S(2)}, u32[]{:S(2)}) %collective-permute-start.2) | collective-permute-done | bytes 15392 | tf_op jit(solution)/shard_map/ppermute | solution.py:167
  8.1 0.0 collective-permute-start.3
  8.1 0.5 collective-permute-start
  8.6 1.0 %collective-permute-done.atm_any.atm_other_s = s32[64]{0:T(128)S(1)} collective-permute-done((s32[64]{0:T(128)}, s32[64]{0:T(128)S(1)}, u32[]{:S(2)}, u32[]{:S(2)}) %collective-permute-start) | collective-permute-done | bytes 288 | tf_op jit(solution)/shard_map/ppermute | solution.py:150
  9.5 0.0 collective-permute-done.3.far
  9.5 6.8 %contribute.1 = (f32[64,16,128]{2,1,0:T(8,128)S(1)}, bf16[64,16,128]{2,1,0:T(8,128)(2,1)S(1)}) custom-call(s32[4,16]{1,0:T(4,128)S(1)} %get-tuple-element.10.nb_s, s32[64]{0:T(128)S(1)} %get-tuple-element.11.src_s, bf16[15,2048]{1,0:T(8,128)(2,1)S(1)} %get-tuple-element.12.own, bf16[15,2048]{1,0:T(8,128)(2,1)S(1)} %collective-permute-done.1.other, ...), custom_call_target="tpu_custom_call" | custom-call | flops 314572800 | bytes 10485760 | tf_op jit(solution)/shard_map/contribute/pallas_call | solution.py:171
  16.3 0.4 collective-permute-start.4
  16.7 1.2 %collective-permute-done.4.recv = bf16[64,16,128]{2,1,0:T(8,128)(2,1)S(1)} collective-permute-done((bf16[64,16,128]{2,1,0:T(8,128)(2,1)S(1)}, bf16[64,16,128]{2,1,0:T(8,128)(2,1)S(1)}, u32[]{:S(2)}, u32[]{:S(2)}) %collective-permute-start.4) | collective-permute-done | bytes 262176 | tf_op jit(solution)/shard_map/ppermute | solution.py:198
  17.9 0.0 copy-done.1
  17.9 0.0 copy-done
  17.9 1.8 %gather_slots.1 = bf16[16,15,16,128]{3,2,1,0:T(8,128)(2,1)S(1)} custom-call(s32[64]{0:T(128)S(1)} %copy-done.1, s32[64]{0:T(128)S(1)} %collective-permute-done.atm_any.atm_other_s, s32[256]{0:T(256)S(1)} %copy-done, f32[64,16,128]{2,1,0:T(8,128)S(1)} %get-tuple-element.13.keep, bf16[64,16,128]{2,1,0:T(8,128)(2,1)S(1)} %collective-permute-done.4.recv), custom_call_target="tpu_custom_call" | custom-call | tf_op jit(solution)/shard_map/gather_slots/pallas_call | solution.py:200
  19.7 32.8 %all_to_all.5.parts = bf16[16,15,16,128]{3,2,1,0:T(8,128)(2,1)S(1)} all-to-all(bf16[16,15,16,128]{3,2,1,0:T(8,128)(2,1)S(1)} %gather_slots.1), channel_id=1, replica_groups=mesh['dom'=16,'field'=2] {'dom'}, dimensions={0} | all-to-all | bytes 1966080 | tf_op jit(solution)/shard_map/all_to_all | solution.py:209
  52.5 0.8 %total.1 = f32[15,2048]{1,0:T(8,128)} custom-call(bf16[16,15,16,128]{3,2,1,0:T(8,128)(2,1)S(1)} %all_to_all.5.parts), custom_call_target="tpu_custom_call" | custom-call | tf_op jit(solution)/shard_map/total/pallas_call | solution.py:210
  (3 shorter events, 0.0 us)
Async XLA Ops:
  0.0 17.9 %copy-start.1 = (s32[64]{0:T(128)S(1)}, s32[64]{0:T(128)}, u32[]{:S(2)}) copy-start(s32[64]{0:T(128)} %atm_s.1) | copy-start | bytes 772
  0.0 17.9 %copy-start = (s32[256]{0:T(256)S(1)}, s32[256]{0:T(256)}, u32[]{:S(2)}) copy-start(s32[256]{0:T(256)} %owner_s.1) | copy-start | bytes 3076
  0.0 1.6 %collective-permute-start.1 = (bf16[15,2048]{1,0:T(8,128)(2,1)}, bf16[15,2048]{1,0:T(8,128)(2,1)S(1)}, u32[]{:S(2)}, u32[]{:S(2)}) collective-permute-start(bf16[15,2048]{1,0:T(8,128)(2,1)} %ocean.1), channel_id=1, source_target_pairs={{0,1},{1,0},{2,3},{3,2},{4,5},{5,4},{6,7},{7,6},{8,9},{9,8},{10,11... | collective-permute-start | bytes 184328 | tf_op jit(solution)/shard_map/ppermute | solution.py:149
  1.6 6.4 %collective-permute-start.2 = (bf16[2,15,256]{2,1,0:T(8,128)(2,1)S(1)}, bf16[2,15,256]{2,1,0:T(8,128)(2,1)S(1)}, u32[]{:S(2)}, u32[]{:S(2)}) collective-permute-start(bf16[2,15,256]{2,1,0:T(8,128)(2,1)S(1)} %pad_maximum_fusion), channel_id=1, source_target_pairs={{0,2},{2,0},{4,6},{6,4},{8,10},{10,8},{12,14},{14,12},{16,18},{18,... | collective-permute-start | bytes 46088 | tf_op jit(solution)/shard_map/ppermute | solution.py:167
  8.1 1.5 %collective-permute-start.3 = (bf16[2,15,256]{2,1,0:T(8,128)(2,1)S(1)}, bf16[2,15,256]{2,1,0:T(8,128)(2,1)S(1)}, u32[]{:S(2)}, u32[]{:S(2)}) collective-permute-start(bf16[2,15,256]{2,1,0:T(8,128)(2,1)S(1)} %collective-permute-done.2.near), channel_id=1, source_target_pairs={{0,1},{1,0},{2,3},{3,2},{4,5},{5,4},{6,7},{7,6},{8,9},{9,8},{10,11... | collective-permute-start | bytes 46088 | tf_op jit(solution)/shard_map/ppermute | solution.py:168
  8.1 1.5 %collective-permute-start = (s32[64]{0:T(128)}, s32[64]{0:T(128)S(1)}, u32[]{:S(2)}, u32[]{:S(2)}) collective-permute-start(s32[64]{0:T(128)} %atm_s.1), channel_id=1, source_target_pairs={{0,1},{1,0},{2,3},{3,2},{4,5},{5,4},{6,7},{7,6},{8,9},{9,8},{10,11... | collective-permute-start | bytes 776 | tf_op jit(solution)/shard_map/ppermute | solution.py:150
  16.3 1.6 %collective-permute-start.4 = (bf16[64,16,128]{2,1,0:T(8,128)(2,1)S(1)}, bf16[64,16,128]{2,1,0:T(8,128)(2,1)S(1)}, u32[]{:S(2)}, u32[]{:S(2)}) collective-permute-start(bf16[64,16,128]{2,1,0:T(8,128)(2,1)S(1)} %get-tuple-element.14), channel_id=1, source_target_pairs={{0,1},{1,0},{2,3},{3,2},{4,5},{5,4},{6,7},{7,6},{8,9},{9,8},{10,11... | collective-permute-start | bytes 786440 | tf_op jit(solution)/shard_map/ppermute | solution.py:198
